TPU v7x, 32 devices: a whole 2x2x4 slice. The times are simulated.
32 devices in a mesh: dp: 4 (over y, x), mp: 8 (over z, core).
Axes of the slice: x: 2, y: 2, z: 4, core: 2. Of those that a mesh axis runs over, the one named last changes fastest.
Arguments:
- tokens: bfloat16 [128, 6144], P(('dp', 'mp')), may hold values from -6 to 6
- norm_gain: float32 [6144], replicated, may hold values from 0.5 to 1.5
- w_query: bfloat16 [6144, 4096], P('dp', 'mp'), as said below
- w_key: bfloat16 [6144, 4096], P('dp', 'mp'), as said below
- w_value: bfloat16 [6144, 4096], P('dp', 'mp'), may hold values from -0.078125 to 0.078125
- w_inner: bfloat16 [6144, 24576], P('dp', 'mp'), may hold values from -0.078125 to 0.078125
- bias_inner: float32 [24576], P('mp'), may hold values from -3 to 3
- w_attn_out: bfloat16 [4096, 6144], P('mp', 'dp'), may hold values from -0.09375 to 0.09375
- w_outer: bfloat16 [24576, 6144], P('mp', 'dp'), may hold values from -0.0390625 to 0.0390625
- temper: float32 [32], P('mp'), may hold values from 0.5 to 24
Outputs:
- result: bfloat16 [128, 6144], P(('dp', 'mp'))
Inputs may be any that keep to these rules, and one draw needn't show every extreme that they name: `w_query`: entries of order 6144 ** -0.5. `w_key`: entries of order 6144 ** -0.5.
All inputs are finite; a program needn't handle non-finite values.
Results may differ from a plain program's by a relative error of at most 0.023.
Values may be sent and summed in bfloat16 or wider, within the bound.
A program may use at most 128 MiB of HBM per device.

v0:
```python
import math
import jax
import jax.numpy as jnp
from jax import lax
from jax.sharding import PartitionSpec as P

HEAD = 128


def normalize(values):
    center = values - jnp.mean(values, axis=-1, keepdims=True)
    spread = jnp.mean(center * center, axis=-1, keepdims=True)
    return center * lax.rsqrt(spread + 1e-06)


def per_device(
    tokens, norm_gain, w_query, w_key, w_value, w_inner, bias_inner, w_attn_out, w_outer, temper
):
    local = tokens.astype(jnp.float32)
    normed = (normalize(local) * norm_gain).astype(jnp.bfloat16)
    image = lax.all_gather(normed, "mp", axis=0, tiled=True)
    count_rows = image.shape[0]
    width_head = w_query.shape[1]
    spread_rows = lax.all_to_all(image, "dp", split_axis=1, concat_axis=0, tiled=True)
    stacked = jnp.concatenate((w_query, w_key, w_value, w_inner), axis=1)
    projected = lax.psum_scatter(
        jnp.dot(spread_rows, stacked, preferred_element_type=jnp.float32).astype(jnp.bfloat16),
        "dp",
        scatter_dimension=0,
        tiled=True,
    ).astype(jnp.float32)
    query_sum = projected[:, :width_head]
    key_sum = projected[:, width_head : 2 * width_head]
    value_sum = projected[:, 2 * width_head : 3 * width_head]
    inner_sum = projected[:, 3 * width_head :]
    heads_dev = width_head // HEAD
    shape = (count_rows, heads_dev, HEAD)
    query_norm = normalize(
        query_sum.astype(jnp.bfloat16).astype(jnp.float32).reshape(shape)
    ).astype(jnp.bfloat16)
    key_norm = normalize(key_sum.astype(jnp.bfloat16).astype(jnp.float32).reshape(shape)).astype(
        jnp.bfloat16
    )
    values = value_sum.astype(jnp.bfloat16).reshape(shape)
    scale = temper / math.sqrt(HEAD)
    scores = jnp.einsum("qhc,khc->hqk", query_norm, key_norm, preferred_element_type=jnp.float32)
    scores = scores * scale[:, None, None]
    probs = jax.nn.softmax(scores, axis=-1).astype(jnp.bfloat16)
    mixed = jnp.einsum("hqk,khc->qhc", probs, values, preferred_element_type=jnp.float32)
    mixed = mixed.astype(jnp.bfloat16).reshape(count_rows, width_head)
    inner = inner_sum + bias_inner
    activ = jax.nn.gelu(inner, approximate=False).astype(jnp.bfloat16)
    attn_full, outer_full = (
        lax.all_gather(w_attn_out, "dp", axis=1, tiled=True),
        lax.all_gather(w_outer, "dp", axis=1, tiled=True),
    )
    attn_part = lax.psum_scatter(
        jnp.dot(mixed, attn_full, preferred_element_type=jnp.float32).astype(jnp.bfloat16),
        "mp",
        scatter_dimension=0,
        tiled=True,
    ).astype(jnp.float32)
    mlp_part = lax.psum_scatter(
        jnp.dot(activ, outer_full, preferred_element_type=jnp.float32).astype(jnp.bfloat16),
        "mp",
        scatter_dimension=0,
        tiled=True,
    ).astype(jnp.float32)
    total = attn_part + mlp_part
    return (local + total).astype(jnp.bfloat16)


def solution(mesh):
    return jax.shard_map(
        per_device,
        mesh=mesh,
        in_specs=(
            P(("dp", "mp"), None),
            P(),
            P("dp", "mp"),
            P("dp", "mp"),
            P("dp", "mp"),
            P("dp", "mp"),
            P("mp"),
            P("mp", "dp"),
            P("mp", "dp"),
            P("mp"),
        ),
        out_specs=P(("dp", "mp"), None),
        check_vma=False,
    )
```

profile of v0, /device:TPU:0, one launch (start us, length us, event | category | flops | bytes accessed | tf_op | source)
XLA Modules:
  0.0 563.7 jit_solution(12790307825521817195)
XLA Ops:
  6.5 1.0 convert_reduce_fusion
  7.5 1.0 fusion.63
  8.5 0.9 fusion.67
  9.5 16.2 %all-gather = bf16[8,4,6144]{2,1,0:T(4,128)(2,1)S(1)} all-gather(bf16[1,4,6144]{2,1,0:T(4,128)(2,1)S(1)} %fusion.67), channel_id=1, replica_groups=mesh['dp'=4,'mp'=8] {'mp'}, dimensions={0}, use_global_device_ids=true | all-gather | bytes 442368 | tf_op jit(solution)/shard_map/all_gather | solution.py:21
  25.7 0.2 all_to_all.14
  26.0 11.1 %all_to_all.19 = bf16[32,4,1536]{2,0,1:T(8,128)(2,1)S(1)} all-to-all(bf16[32,4,1536]{2,0,1:T(8,128)(2,1)S(1)} %copy.32), channel_id=1, replica_groups=mesh['dp'=4,'mp'=8] {'dp'}, dimensions={1} | all-to-all | bytes 786432 | tf_op jit(solution)/shard_map/all_to_all | solution.py:24
  37.2 8.7 %fusion.9 = bf16[128,4608]{1,0:T(8,128)(2,1)} fusion(bf16[128,1536]{1,0:T(8,128)(2,1)S(1)} %bitcast.20, bf16[1536,3072]{1,0:T(8,128)(2,1)} %param.15, bf16[1536,512]{1,0:T(8,128)(2,1)} %param.14, bf16[1536,512]{1,0:T(8,128)(2,1)} %param.13, bf16[1536,512]{1,0:T(8,128)(2,1)} %param.12), kind=kOutput, calls=%fused_computation.11 | convolution fusion | flops 1869152256 | bytes 15728640 | tf_op jit(solution)/shard_map/dot_general | solution.py:27
  45.9 0.7 all-gather.4.cloned.1.call-update
  46.7 0.7 all-gather.6.cloned.1.call-update
  47.4 26.8 %reduce-scatter.2.cloned.1.call-done = bf16[32,4608]{1,0:T(8,128)(2,1)} async-done(((bf16[128,4608]{1,0:T(8,128)(2,1)}), bf16[32,4608]{1,0:T(8,128)(2,1)}) %reduce-scatter.2.cloned.1.call-update) | async-done | bytes 294928 | tf_op jit(solution)/shard_map/reduce_scatter | solution.py:26
  74.3 0.8 slice_bitcast_fusion
  75.1 0.1 reduce_sum.65
  75.4 0.2 multiply_reduce_fusion.1
  75.6 0.2 multiply_reduce_fusion
  75.8 0.2 multiply_convert_fusion
  76.0 0.2 fusion.110
  76.2 0.2 fusion.14
  76.4 69.8 %all-gather.4.cloned.1.call-done = bf16[512,6144]{1,0:T(8,128)(2,1)} async-done(((bf16[512,1536]{1,0:T(8,128)(2,1)}), bf16[512,6144]{1,0:T(8,128)(2,1)}) %all-gather.4.cloned.1.call-update) | async-done | bytes 6291472 | tf_op jit(solution)/shard_map/all_gather | solution.py:54
  146.2 4.7 convolution_convert_fusion.1
  150.9 330.0 %all-gather.6.cloned.1.call-done = bf16[3072,6144]{1,0:T(8,128)(2,1)} async-done(((bf16[3072,1536]{1,0:T(8,128)(2,1)}), bf16[3072,6144]{1,0:T(8,128)(2,1)}) %all-gather.6.cloned.1.call-update) | async-done | bytes 37748752 | tf_op jit(solution)/shard_map/all_gather | solution.py:55
  480.9 16.6 %convolution_convert_fusion = bf16[32,6144]{1,0:T(8,128)(2,1)} fusion(bf16[3072,6144]{1,0:T(8,128)(2,1)} %all-gather.6.cloned.1.call-done, bf16[32,4608]{1,0:T(8,128)(2,1)} %reduce-scatter.2.cloned.1.call-done, f32[3072]{0:T(1024)S(1)} %copy-done.1), kind=kOutput, calls=%fused_computation.9 | convolution fusion | flops 1214742528 | bytes 38350848 | tf_op jit(solution)/shard_map/dot_general | solution.py:64
  497.5 0.6 dynamic-slice
  498.8 56.7 %all-reduce.5.cloned.1.call-done = (bf16[32,6144]{1,0:T(8,128)(2,1)}, bf16[32,6144]{1,0:T(8,128)(2,1)}) async-done(((bf16[32,6144]{1,0:T(8,128)(2,1)}, bf16[32,6144]{1,0:T(8,128)(2,1)}), (bf16[32,6144]{1,0:T(8,128)(2,1)}, bf16[32,6144]{1,0:T(8,128)(2,1)})) %all-reduce.5.cloned.1.call-update) | async-done | bytes 786448
  555.5 1.6 fusion.66
  (25 shorter events, 0.4 us)
Async XLA Ops:
  6.5 67.7 %reduce-scatter.2.cloned.1.call-start = ((), (), s32[]{:S(2)}) async-start(), calls=%async_computation.2 | async-start | bytes 1474560 | tf_op jit(solution)/shard_map/reduce_scatter | solution.py:26
  45.8 1.6 copy-start.2
  45.9 435.1 %copy-start.1 = (f32[3072]{0:T(1024)S(1)}, f32[3072]{0:T(1024)}, u32[]{:S(2)}) copy-start(f32[3072]{0:T(1024)} %param.16) | copy-start | bytes 36868
  45.9 100.3 %all-gather.4.cloned.1.call-start = ((), (), s32[]{:S(2)}) async-start(), calls=%async_computation.3 | async-start | bytes 7864320 | tf_op jit(solution)/shard_map/all_gather | solution.py:54
  46.6 434.3 %all-gather.6.cloned.1.call-start = ((), (), s32[]{:S(2)}) async-start(), calls=%async_computation.4 | async-start | bytes 47185920 | tf_op jit(solution)/shard_map/all_gather | solution.py:55
  47.4 508.1 %all-reduce.5.cloned.1.call-start = ((), (), s32[]{:S(2)}) async-start(), calls=%async_computation.5 | async-start | bytes 1572864
  150.9 346.6 %copy-start.3 = (u32[32]{0:T(128)S(1)}, u32[32]{0:T(128)}, u32[]{:S(2)}) copy-start(u32[32]{0:T(128)} %constant.84) | copy-start | bytes 388
  150.9 404.6 %copy-start = (bf16[4,6144]{1,0:T(4,128)(2,1)S(1)}, bf16[4,6144]{1,0:T(4,128)(2,1)}, u32[]{:S(2)}) copy-start(bf16[4,6144]{1,0:T(4,128)(2,1)} %param.10) | copy-start | bytes 147460
Sparse Core Ops, SparseCore 0:
  46.0 28.2 reduce-scatter.1
  76.1 70.0 all-gather.3
  148.0 332.8 all-gather.5
  497.6 57.8 all-reduce.4
where the time goes:
time: 564 us
  waiting for transfers between devices  485 us (86%)
  matrix products  30.4 us (5%)
  blocking collectives  27.4 us (5%)
  between operations  13.9 us (2%)
  other arithmetic  6.14 us (1%)
    all_gather x1, waiting for transfers between devices, per_device(): lax.all_gather(w_outer, 'dp', axis=1, tiled=True)  330 us
    all_gather x1, waiting for transfers between devices, per_device(): lax.all_gather(w_attn_out, 'dp', axis=1, tiled=True)  69.8 us
    unnamed x5, waiting for transfers between devices  58.1 us
    reduce_scatter x1, waiting for transfers between devices, per_device(): lax.psum_scatter(jnp.dot(spread_rows, stacked, preferred_element_type=jnp...  26.8 us
    dot_general x1, matrix products, per_device(): jnp.dot(activ, outer_full, preferred_element_type=jnp.float32)  16.6 us
    all_gather x1, blocking collectives, per_device(): image = lax.all_gather(normed, 'mp', axis=0, tiled=True)  16.2 us
  transfers between devices with their start and end apart: 4, of which 4 were waited for; matrix products, arithmetic and copies ran while one was open for 1% of the time, Pallas kernels for 0%

commit v1 on v0

--- a/solution.py
+++ b/solution.py
@@ -52,7 +52,7 @@
     activ = jax.nn.gelu(inner, approximate=False).astype(jnp.bfloat16)
     attn_full, outer_full = (
         lax.all_gather(w_attn_out, "dp", axis=1, tiled=True),
-        lax.all_gather(w_outer, "dp", axis=1, tiled=True),
+        jnp.concatenate(lax.all_gather(w_outer, "dp"), axis=1),
     )
     attn_part = lax.psum_scatter(
         jnp.dot(mixed, attn_full, preferred_element_type=jnp.float32).astype(jnp.bfloat16),

time: 564 us -> 615 us (1.090)
  local copies, waits for them, and re-layouts: 0.97 us -> 49.7 us
    reshape x0 -> x1, local copies, waits for them, and re-layouts: none -> 48.7 us  [per_device(): jnp.concatenate(lax.all_gather(w_outer, 'dp'), axis=1)]
where the time goes in v1:
time: 615 us; the launch traced here: 613 us
  waiting for transfers between devices  485 us (79%)
  local copies, waits for them, and re-layouts  49.7 us (8%)
  matrix products  31.4 us (5%)
  blocking collectives  27.4 us (4%)
  between operations  13.9 us (2%)
    all_gather x1, waiting for transfers between devices, per_device(): lax.all_gather(w_outer, 'dp')  330 us
    all_gather x1, waiting for transfers between devices, per_device(): lax.all_gather(w_attn_out, 'dp', axis=1, tiled=True)  69.8 us
    unnamed x5, waiting for transfers between devices  58.1 us
    reshape x1, local copies, waits for them, and re-layouts, per_device(): jnp.concatenate(lax.all_gather(w_outer, 'dp'), axis=1)  48.7 us
    reduce_scatter x1, waiting for transfers between devices, per_device(): lax.psum_scatter(jnp.dot(spread_rows, stacked, preferred_element_type=jnp...  26.8 us
    dot_general x1, matrix products, per_device(): jnp.dot(activ, outer_full, preferred_element_type=jnp.float32)  17.6 us
    all_gather x1, blocking collectives, per_device(): image = lax.all_gather(normed, 'mp', axis=0, tiled=True)  16.2 us
  transfers between devices with their start and end apart: 4, of which 4 were waited for; matrix products, arithmetic and copies ran while one was open for 1% of the time, Pallas kernels for 0%

profile of v1, /device:TPU:0, one launch (start us, length us, event | category | flops | bytes accessed | tf_op | source)
XLA Modules:
  0.0 613.5 jit_solution(9946589408042642868)
XLA Ops:
  6.5 1.0 convert_reduce_fusion
  7.5 1.0 fusion.63
  8.5 0.9 fusion.67
  9.5 16.2 %all-gather.1 = bf16[8,4,6144]{2,1,0:T(4,128)(2,1)S(1)} all-gather(bf16[1,4,6144]{2,1,0:T(4,128)(2,1)S(1)} %fusion.67), channel_id=1, replica_groups=mesh['dp'=4,'mp'=8] {'mp'}, dimensions={0}, use_global_device_ids=true | all-gather | bytes 442368 | tf_op jit(solution)/shard_map/all_gather | solution.py:21
  25.7 0.2 all_to_all.14
  26.0 11.1 %all_to_all.19 = bf16[32,4,1536]{2,0,1:T(8,128)(2,1)S(1)} all-to-all(bf16[32,4,1536]{2,0,1:T(8,128)(2,1)S(1)} %copy.41), channel_id=1, replica_groups=mesh['dp'=4,'mp'=8] {'dp'}, dimensions={1} | all-to-all | bytes 786432 | tf_op jit(solution)/shard_map/all_to_all | solution.py:24
  37.2 8.7 %fusion.9 = bf16[128,4608]{1,0:T(8,128)(2,1)} fusion(bf16[128,1536]{1,0:T(8,128)(2,1)S(1)} %bitcast.26, bf16[1536,3072]{1,0:T(8,128)(2,1)} %param.15, bf16[1536,512]{1,0:T(8,128)(2,1)} %param.14, bf16[1536,512]{1,0:T(8,128)(2,1)} %param.13, bf16[1536,512]{1,0:T(8,128)(2,1)} %param.12), kind=kOutput, calls=%fused_computation.11 | convolution fusion | flops 1869152256 | bytes 15728640 | tf_op jit(solution)/shard_map/dot_general | solution.py:27
  45.9 0.7 all-gather.5.cloned.1.call-update
  46.7 0.7 all-gather.7.cloned.1.call-update
  47.4 26.8 %reduce-scatter.2.cloned.1.call-done = bf16[32,4608]{1,0:T(8,128)(2,1)} async-done(((bf16[128,4608]{1,0:T(8,128)(2,1)}), bf16[32,4608]{1,0:T(8,128)(2,1)}) %reduce-scatter.2.cloned.1.call-update) | async-done | bytes 294928 | tf_op jit(solution)/shard_map/reduce_scatter | solution.py:26
  74.3 0.8 slice_bitcast_fusion
  75.4 0.2 multiply_reduce_fusion
  75.6 0.2 multiply_reduce_fusion.1
  75.8 0.2 multiply_convert_fusion
  76.0 0.2 fusion.110
  76.2 0.2 fusion.14
  76.4 69.8 %all-gather.5.cloned.1.call-done = bf16[512,6144]{1,0:T(8,128)(2,1)} async-done(((bf16[512,1536]{1,0:T(8,128)(2,1)}), bf16[512,6144]{1,0:T(8,128)(2,1)}) %all-gather.5.cloned.1.call-update) | async-done | bytes 6291472 | tf_op jit(solution)/shard_map/all_gather | solution.py:54
  146.2 4.7 convolution_convert_fusion.1
  150.9 330.0 %all-gather.7.cloned.1.call-done = bf16[12288,1536]{1,0:T(8,128)(2,1)} async-done(((bf16[3072,1536]{1,0:T(8,128)(2,1)}), bf16[12288,1536]{1,0:T(8,128)(2,1)}) %all-gather.7.cloned.1.call-update) | async-done | bytes 37748752 | tf_op jit(solution)/shard_map/all_gather | solution.py:55
  481.0 48.7 %copy.47 = bf16[3072,4,1536]{0,2,1:T(8,128)(2,1)} copy(bf16[3072,4,1536]{2,0,1:T(8,128)(2,1)} %bitcast.25) | data formatting | bytes 75497472 | tf_op jit(solution)/shard_map/reshape | solution.py:55
  529.7 17.6 %convolution_convert_fusion = bf16[32,6144]{1,0:T(8,128)(2,1)} fusion(bf16[3072,6144]{0,1:T(8,128)(2,1)} %bitcast.24, bf16[32,4608]{1,0:T(8,128)(2,1)S(1)} %copy-done.1, f32[3072]{0:T(1024)S(1)} %copy-done.2), kind=kOutput, calls=%fused_computation.9 | convolution fusion | flops 1214742528 | bytes 38350848 | tf_op jit(solution)/shard_map/dot_general | solution.py:64
  547.4 0.6 dynamic-slice
  548.6 56.7 %all-reduce.5.cloned.1.call-done = (bf16[32,6144]{1,0:T(8,128)(2,1)}, bf16[32,6144]{1,0:T(8,128)(2,1)}) async-done(((bf16[32,6144]{1,0:T(8,128)(2,1)}, bf16[32,6144]{1,0:T(8,128)(2,1)}), (bf16[32,6144]{1,0:T(8,128)(2,1)}, bf16[32,6144]{1,0:T(8,128)(2,1)})) %all-reduce.5.cloned.1.call-update) | async-done | bytes 786448
  605.3 1.6 fusion.66
  (28 shorter events, 0.5 us)
Async XLA Ops:
  6.5 67.7 %reduce-scatter.2.cloned.1.call-start = ((), (), s32[]{:S(2)}) async-start(), calls=%async_computation.2 | async-start | bytes 1474560 | tf_op jit(solution)/shard_map/reduce_scatter | solution.py:26
  45.8 1.6 copy-start.3
  45.9 100.3 %all-gather.5.cloned.1.call-start = ((), (), s32[]{:S(2)}) async-start(), calls=%async_computation.3 | async-start | bytes 7864320 | tf_op jit(solution)/shard_map/all_gather | solution.py:54
  46.6 434.3 %all-gather.7.cloned.1.call-start = ((), (), s32[]{:S(2)}) async-start(), calls=%async_computation.4 | async-start | bytes 47185920 | tf_op jit(solution)/shard_map/all_gather | solution.py:55
  47.4 558.0 %all-reduce.5.cloned.1.call-start = ((), (), s32[]{:S(2)}) async-start(), calls=%async_computation.5 | async-start | bytes 1572864
  481.0 48.7 %copy-start.1 = (bf16[32,4608]{1,0:T(8,128)(2,1)S(1)}, bf16[32,4608]{1,0:T(8,128)(2,1)}, u32[]{:S(2)}) copy-start(bf16[32,4608]{1,0:T(8,128)(2,1)} %reduce-scatter.2.cloned.1.call-done) | copy-start | bytes 884740
  481.0 48.7 %copy-start.2 = (f32[3072]{0:T(1024)S(1)}, f32[3072]{0:T(1024)}, u32[]{:S(2)}) copy-start(f32[3072]{0:T(1024)} %param.16) | copy-start | bytes 36868
  529.7 17.7 %copy-start.4 = (u32[32]{0:T(128)S(1)}, u32[32]{0:T(128)}, u32[]{:S(2)}) copy-start(u32[32]{0:T(128)} %constant.84) | copy-start | bytes 388
  529.7 75.6 %copy-start = (bf16[4,6144]{1,0:T(4,128)(2,1)S(1)}, bf16[4,6144]{1,0:T(4,128)(2,1)}, u32[]{:S(2)}) copy-start(bf16[4,6144]{1,0:T(4,128)(2,1)} %param.10) | copy-start | bytes 147460
Sparse Core Ops, SparseCore 0:
  46.0 28.2 reduce-scatter.1
  76.1 70.0 all-gather.4
  148.1 332.8 all-gather.6
  547.5 57.8 all-reduce.4

commit v2 on v0

--- a/solution.py
+++ b/solution.py
@@ -51,7 +51,9 @@
     inner = inner_sum + bias_inner
     activ = jax.nn.gelu(inner, approximate=False).astype(jnp.bfloat16)
     attn_full, outer_full = (
-        lax.all_gather(w_attn_out, "dp", axis=1, tiled=True),
+        jnp.concatenate(
+            lax.all_to_all(jnp.stack([w_attn_out] * lax.axis_size("dp")), "dp", 0, 0), axis=1
+        ),
         lax.all_gather(w_outer, "dp", axis=1, tiled=True),
     )
     attn_part = lax.psum_scatter(

time: 564 us -> 551 us (0.977)
  waiting for transfers between devices: 485 us -> 461 us
    all_gather x1 -> x0, waiting for transfers between devices: 69.8 us -> none  [per_device(): lax.all_gather(w_attn_out, 'dp', axis=1, tiled=True)]
    reduce_scatter x1, waiting for transfers between devices: 26.8 us -> 56.4 us  [per_device(): lax.psum_scatter(jnp.dot(spread_rows, stacked, preferred_element_type=jnp...]
    all_to_all x0 -> x1, waiting for transfers between devices: none -> 16.5 us  [per_device(): lax.all_to_all(jnp.stack([w_attn_out] * lax.axis_size('dp')), 'dp', 0, 0)]
    unnamed x5 -> x4, waiting for transfers between devices: 58.1 us -> 57.5 us
  transfers between devices with their start and end apart: 4 -> 4, of which waited for: 4 -> 4; matrix products, arithmetic and copies ran while one was open for 1% -> 2% of each run, Pallas kernels for 0% -> 0%
where the time goes in v2:
time: 551 us; the launch traced here: 550 us
  waiting for transfers between devices  461 us (84%)
  matrix products  31.1 us (6%)
  blocking collectives  27.4 us (5%)
  between operations  13.9 us (3%)
  other arithmetic  6.14 us (1%)
    all_gather x1, waiting for transfers between devices, per_device(): lax.all_gather(w_outer, 'dp', axis=1, tiled=True)  330 us
    unnamed x4, waiting for transfers between devices  57.5 us
    reduce_scatter x1, waiting for transfers between devices, per_device(): lax.psum_scatter(jnp.dot(spread_rows, stacked, preferred_element_type=jnp...  56.4 us
    dot_general x1, matrix products, per_device(): jnp.dot(activ, outer_full, preferred_element_type=jnp.float32)  16.6 us
    all_to_all x1, waiting for transfers between devices, per_device(): lax.all_to_all(jnp.stack([w_attn_out] * lax.axis_size('dp')), 'dp', 0, 0)  16.5 us
    all_gather x1, blocking collectives, per_device(): image = lax.all_gather(normed, 'mp', axis=0, tiled=True)  16.2 us
    all_to_all x1, blocking collectives, per_device(): lax.all_to_all(image, 'dp', split_axis=1, concat_axis=0, tiled=True)  11.1 us
  transfers between devices with their start and end apart: 4, of which 4 were waited for; matrix products, arithmetic and copies ran while one was open for 2% of the time, Pallas kernels for 0%

profile of v2, /device:TPU:0, one launch (start us, length us, event | category | flops | bytes accessed | tf_op | source)
XLA Modules:
  0.0 550.1 jit_solution(17703773488470072747)
XLA Ops:
  6.5 1.0 convert_reduce_fusion
  7.5 1.0 fusion.63
  8.5 0.9 fusion.67
  9.5 16.2 %all-gather = bf16[8,4,6144]{2,1,0:T(4,128)(2,1)S(1)} all-gather(bf16[1,4,6144]{2,1,0:T(4,128)(2,1)S(1)} %fusion.67), channel_id=1, replica_groups=mesh['dp'=4,'mp'=8] {'mp'}, dimensions={0}, use_global_device_ids=true | all-gather | bytes 442368 | tf_op jit(solution)/shard_map/all_gather | solution.py:21
  25.7 0.2 all_to_all.17
  26.0 11.1 %all_to_all.24 = bf16[32,4,1536]{2,0,1:T(8,128)(2,1)S(1)} all-to-all(bf16[32,4,1536]{2,0,1:T(8,128)(2,1)S(1)} %copy.35), channel_id=1, replica_groups=mesh['dp'=4,'mp'=8] {'dp'}, dimensions={1} | all-to-all | bytes 786432 | tf_op jit(solution)/shard_map/all_to_all | solution.py:24
  37.2 8.7 %fusion.9 = bf16[128,4608]{1,0:T(8,128)(2,1)} fusion(bf16[128,1536]{1,0:T(8,128)(2,1)S(1)} %bitcast.23, bf16[1536,3072]{1,0:T(8,128)(2,1)} %param.15, bf16[1536,512]{1,0:T(8,128)(2,1)} %param.14, bf16[1536,512]{1,0:T(8,128)(2,1)} %param.13, bf16[1536,512]{1,0:T(8,128)(2,1)} %param.12), kind=kOutput, calls=%fused_computation.11 | convolution fusion | flops 1869152256 | bytes 15728640 | tf_op jit(solution)/shard_map/dot_general | solution.py:27
  45.9 0.7 all-gather.3.cloned.1.call-update
  46.6 0.6 copy-done
  47.3 0.7 copy.41
  48.0 3.1 stack.2
  51.0 5.4 all-to-all-start.1
  56.5 56.4 %reduce-scatter.2.cloned.1.call-done = bf16[32,4608]{1,0:T(8,128)(2,1)} async-done(((bf16[128,4608]{1,0:T(8,128)(2,1)}), bf16[32,4608]{1,0:T(8,128)(2,1)}) %reduce-scatter.2.cloned.1.call-update) | async-done | bytes 294928 | tf_op jit(solution)/shard_map/reduce_scatter | solution.py:26
  112.9 0.8 slice_bitcast_fusion
  114.0 0.2 multiply_reduce_fusion
  114.4 0.2 multiply_convert_fusion
  114.8 0.2 fusion.14
  115.0 16.5 %all-to-all-done.1 = bf16[4,512,1536]{1,2,0:T(8,128)(2,1)} async-done(((bf16[4,512,1536]{1,2,0:T(8,128)(2,1)}), bf16[4,512,1536]{1,2,0:T(8,128)(2,1)}, u32[]{:S(2)}, u32[]{:S(2)}) %all-to-all-start.1) | async-done | bytes 6291488 | tf_op jit(solution)/shard_map/all_to_all | solution.py:55
  131.5 5.5 convolution_convert_fusion.1
  137.0 330.4 %all-gather.3.cloned.1.call-done = bf16[3072,6144]{1,0:T(8,128)(2,1)} async-done(((bf16[3072,1536]{1,0:T(8,128)(2,1)}), bf16[3072,6144]{1,0:T(8,128)(2,1)}) %all-gather.3.cloned.1.call-update) | async-done | bytes 37748752 | tf_op jit(solution)/shard_map/all_gather | solution.py:57
  467.4 16.6 %convolution_convert_fusion = bf16[32,6144]{1,0:T(8,128)(2,1)} fusion(bf16[3072,6144]{1,0:T(8,128)(2,1)} %all-gather.3.cloned.1.call-done, bf16[32,4608]{1,0:T(8,128)(2,1)} %reduce-scatter.2.cloned.1.call-done, f32[3072]{0:T(1024)S(1)} %copy-done.2), kind=kOutput, calls=%fused_computation.9 | convolution fusion | flops 1214742528 | bytes 38350848 | tf_op jit(solution)/shard_map/dot_general | solution.py:66
  484.0 0.6 dynamic-slice
  485.2 56.7 %all-reduce.5.cloned.1.call-done = (bf16[32,6144]{1,0:T(8,128)(2,1)}, bf16[32,6144]{1,0:T(8,128)(2,1)}) async-done(((bf16[32,6144]{1,0:T(8,128)(2,1)}, bf16[32,6144]{1,0:T(8,128)(2,1)}), (bf16[32,6144]{1,0:T(8,128)(2,1)}, bf16[32,6144]{1,0:T(8,128)(2,1)})) %all-reduce.5.cloned.1.call-update) | async-done | bytes 786448
  542.0 1.6 fusion.66
  (28 shorter events, 0.9 us)
Async XLA Ops:
  6.5 106.4 %reduce-scatter.2.cloned.1.call-start = ((), (), s32[]{:S(2)}) async-start(), calls=%async_computation.3 | async-start | bytes 1474560 | tf_op jit(solution)/shard_map/reduce_scatter | solution.py:26
  45.8 1.4 copy-start
  45.9 421.5 %all-gather.3.cloned.1.call-start = ((), (), s32[]{:S(2)}) async-start(), calls=%async_computation.4 | async-start | bytes 47185920 | tf_op jit(solution)/shard_map/all_gather | solution.py:57
  48.0 8.5 %copy-start.3 = (f32[4]{0:T(128)S(1)}, f32[4]{0:T(128)}, u32[]{:S(2)}) copy-start(f32[4]{0:T(128)} %param.19) | copy-start | bytes 52
  51.0 416.4 %copy-start.2 = (f32[3072]{0:T(1024)S(1)}, f32[3072]{0:T(1024)}, u32[]{:S(2)}) copy-start(f32[3072]{0:T(1024)} %param.16) | copy-start | bytes 36868
  51.0 80.5 %all-to-all-start.1 = ((bf16[4,512,1536]{1,2,0:T(8,128)(2,1)}), bf16[4,512,1536]{1,2,0:T(8,128)(2,1)}, u32[]{:S(2)}, u32[]{:S(2)}) async-start(bf16[4,512,1536]{1,2,0:T(8,128)(2,1)} %stack.2), calls=%async_computation.2 | async-start | bytes 12582912 | tf_op jit(solution)/shard_map/all_to_all | solution.py:55
  56.4 485.6 %all-reduce.5.cloned.1.call-start = ((), (), s32[]{:S(2)}) async-start(), calls=%async_computation.5 | async-start | bytes 1572864
  137.0 347.0 %copy-start.4 = (u32[32]{0:T(128)S(1)}, u32[32]{0:T(128)}, u32[]{:S(2)}) copy-start(u32[32]{0:T(128)} %constant.84) | copy-start | bytes 388
  137.0 405.0 %copy-start.1 = (bf16[4,6144]{1,0:T(4,128)(2,1)S(1)}, bf16[4,6144]{1,0:T(4,128)(2,1)}, u32[]{:S(2)}) copy-start(bf16[4,6144]{1,0:T(4,128)(2,1)} %param.10) | copy-start | bytes 147460
Sparse Core Ops, SparseCore 0:
  46.0 66.8 reduce-scatter.1
  114.8 352.5 all-gather.2
  484.1 57.8 all-reduce.4
